TPU v7x, 32 devices: a whole 2x2x4 slice. The times are simulated.
32 devices in a mesh: dp: 2 (over x), tp: 4 (over z), section: 4 (over y, core).
Axes of the slice: x: 2, y: 2, z: 4, core: 2. Of those that a mesh axis runs over, the one named last changes fastest.
Arguments:
- tokens: bfloat16 [256, 2304], P('dp', 'section'), may hold values from -6 to 6
- hidden_grad: bfloat16 [256, 18432], P('dp', ('tp', 'section')), may hold values from -6 to 6
- norm_gain: float32 [2304], replicated, may hold values from 0.5 to 1.5
- w_gate: bfloat16 [2304, 18432], P('dp', ('tp', 'section')), may hold values from -0.125 to 0.125
- w_up: bfloat16 [2304, 18432], P('dp', ('tp', 'section')), may hold values from -0.125 to 0.125
Outputs:
- grad_tokens: bfloat16 [256, 2304], P('dp', ('tp', 'section'))
- grad_gain: float32 [2304], P(('tp', 'section'))
- grad_gate: bfloat16 [2304, 18432], P('dp', ('tp', 'section'))
- grad_up: bfloat16 [2304, 18432], P('dp', ('tp', 'section'))
All inputs are finite; a program needn't handle non-finite values.
Results may differ from a plain program's by a relative error of at most 0.018.
Values may be sent and summed in bfloat16 or wider, within the bound.
A program may use at most 128 MiB of HBM per device.

v0:
```python
import jax
import jax.numpy as jnp
from jax import lax
from jax.sharding import PartitionSpec as P

D = 2304
epsilon = 1e-06


def gated_unit(gate, up):
    return jax.nn.gelu(gate, approximate=True) * up


def shards(tokens, hidden_grad, norm_gain, w_gate, w_up):
    rows_in = lax.all_gather(tokens, "section", axis=1, tiled=True)
    inputs = rows_in.astype(jnp.float32)
    inv_rms = lax.rsqrt(jnp.mean(inputs * inputs, axis=1) + epsilon)
    normed = (inputs * inv_rms[:, None] * norm_gain).astype(jnp.bfloat16)
    full_gate, full_up = (
        lax.all_gather(w_gate, "dp", axis=0, tiled=True),
        lax.all_gather(w_up, "dp", axis=0, tiled=True),
    )
    gate = jnp.dot(normed, full_gate, preferred_element_type=jnp.float32)
    up = jnp.dot(normed, full_up, preferred_element_type=jnp.float32)
    hidden, pull = jax.vjp(gated_unit, gate, up)
    d_gate, d_up = pull(hidden_grad.astype(jnp.float32))
    d_gate = d_gate.astype(jnp.bfloat16)
    d_up = d_up.astype(jnp.bfloat16)
    contract_cols = (((1,), (1,)), ((), ()))
    contract_rows = (((0,), (0,)), ((), ()))
    features = full_gate.shape[0]
    own_width = features // lax.axis_size(("tp", "section"))
    first = lax.dot_general(full_gate, d_gate, contract_cols, preferred_element_type=jnp.float32)
    second = lax.dot_general(full_up, d_up, contract_cols, preferred_element_type=jnp.float32)
    d_columns = lax.psum_scatter(
        (first + second).astype(jnp.bfloat16), ("tp", "section"), scatter_dimension=0, tiled=True
    ).astype(jnp.float32)
    d_normed = d_columns.T
    offset = lax.axis_index(("tp", "section")) * own_width
    own_inputs = lax.dynamic_slice_in_dim(inputs, offset, own_width, 1)
    own_gain = lax.dynamic_slice_in_dim(norm_gain, offset, own_width, 0)
    gain_part = jnp.sum(d_normed * own_inputs * inv_rms[:, None], axis=0)
    row_part = jnp.sum(own_inputs * own_gain * d_normed, axis=1)
    grad_gain = lax.psum(gain_part, "dp")
    row_sum = lax.psum(row_part, ("tp", "section"))
    grad_tokens = (
        inv_rms[:, None] * own_gain * d_normed - own_inputs * (inv_rms**3 * row_sum / D)[:, None]
    )
    block = w_gate.shape[0]
    fwidth = w_gate.shape[1]
    cols_normed = lax.all_to_all(normed, "dp", split_axis=1, concat_axis=0, tiled=True)
    per_device = normed.shape[0]
    empty = jnp.zeros((block, fwidth), jnp.float32)
    piece_gate = lax.all_gather(d_gate, "dp", axis=0, tiled=True)
    piece_up = lax.all_gather(d_up, "dp", axis=0, tiled=True)

    def one_block(index, running):
        inner = index * per_device
        block_normed = lax.dynamic_slice_in_dim(cols_normed, inner, per_device, 0)
        block_gate = lax.dynamic_slice_in_dim(piece_gate, inner, per_device, 0)
        block_up = lax.dynamic_slice_in_dim(piece_up, inner, per_device, 0)
        terms = (
            lax.dot_general(
                block_normed, block_gate, contract_rows, preferred_element_type=jnp.float32
            ),
            lax.dot_general(
                block_normed, block_up, contract_rows, preferred_element_type=jnp.float32
            ),
        )
        return tuple(
            (
                total + lax.optimization_barrier(term.astype(jnp.bfloat16)).astype(jnp.float32)
                for total, term in zip(running, terms)
            )
        )

    sum_gate, sum_up = lax.fori_loop(
        0, piece_gate.shape[0] // per_device, one_block, (empty, empty)
    )
    return (
        grad_tokens.astype(jnp.bfloat16),
        grad_gain,
        sum_gate.astype(jnp.bfloat16),
        sum_up.astype(jnp.bfloat16),
    )


def solution(mesh):
    in_specs = (
        P("dp", "section"),
        P("dp", ("tp", "section")),
        P(),
        P("dp", ("tp", "section")),
        P("dp", ("tp", "section")),
    )
    out_specs = (
        P("dp", ("tp", "section")),
        P(("tp", "section")),
        P("dp", ("tp", "section")),
        P("dp", ("tp", "section")),
    )
    return jax.shard_map(shards, mesh=mesh, in_specs=in_specs, out_specs=out_specs, check_vma=False)
```

profile of v0, /device:TPU:0, one launch (start us, length us, event | category | flops | bytes accessed | tf_op | source)
XLA Modules:
  0.0 266.3 jit_solution(6498756828406113752)
XLA Ops:
  7.2 0.0 copy-start.3
  7.2 0.0 copy-start.4
  7.2 0.0 all-gather.5.cloned.1.call-start
  7.2 0.7 all-gather.5.cloned.1.call-update
  7.9 0.0 copy-start.2
  7.9 0.0 all-gather.3.cloned.1.call-start
  8.0 0.7 all-gather.3.cloned.1.call-update
  8.7 0.0 copy-done.3
  8.7 9.0 %all_gather.15 = bf16[128,2304]{0,1:T(8,128)(2,1)S(1)} all-gather(bf16[128,576]{0,1:T(8,128)(2,1)S(1)} %copy-done.3), channel_id=1, replica_groups=mesh['dp'=2,'tp'=4,'section'=4] {'section'}, dimensions={1}, use_global_device_ids=true | all-gather | bytes 737280 | tf_op jit(solution)/shard_map/all_gather | solution.py:15
  17.7 0.3 multiply_reduce_fusion
  18.1 0.0 copy-done.4
  18.1 0.4 multiply_convert_fusion
  18.4 1.1 copy.13
  19.5 3.5 %all-to-all-start = ((bf16[128,2,1152]{2,0,1:T(8,128)(2,1)}), bf16[128,2,1152]{2,0,1:T(8,128)(2,1)S(1)}, u32[]{:S(2)}, u32[]{:S(2)}) async-start(bf16[128,2,1152]{2,0,1:T(8,128)(2,1)} %copy.13), calls=%async_computation | async-start | bytes 1179648 | tf_op jit(solution)/shard_map/all_to_all | solution.py:51
  23.0 0.0 reduce-scatter.4.cloned.1.call-start
  23.1 1.1 convert_element_type.59
  24.2 0.1 dynamic_slice.27
  24.3 63.6 %all-gather.5.cloned.1.call-done = bf16[2304,1152]{1,0:T(8,128)(2,1)} async-done(((bf16[1152,1152]{1,0:T(8,128)(2,1)}), bf16[2304,1152]{1,0:T(8,128)(2,1)}) %all-gather.5.cloned.1.call-update) | async-done | bytes 5308432 | tf_op jit(solution)/shard_map/all_gather | solution.py:20
  87.9 0.0 copy-done.2
  87.9 3.7 %fusion.8 = (bf16[128,1152]{1,0:T(8,128)(2,1)S(1)}, f32[128,1152]{1,0:T(8,128)S(1)}) fusion(bf16[128,1152]{1,0:T(8,128)(2,1)S(1)} %copy-done.2, bf16[128,2304]{0,1:T(8,128)(2,1)S(1)} %multiply_convert_fusion, bf16[2304,1152]{1,0:T(8,128)(2,1)} %all-gather.5.cloned.1.call-done), kind=kOutput, calls=%fused_computation.19 | convolution fusion | flops 681099264 | bytes 7077888 | tf_op jit(solution)/shard_map/dot_general | solution.py:23
  91.6 67.1 %all-gather.3.cloned.1.call-done = bf16[2304,1152]{1,0:T(8,128)(2,1)} async-done(((bf16[1152,1152]{1,0:T(8,128)(2,1)}), bf16[2304,1152]{1,0:T(8,128)(2,1)}) %all-gather.3.cloned.1.call-update) | async-done | bytes 5308432 | tf_op jit(solution)/shard_map/all_gather | solution.py:21
  158.7 4.0 %fusion.15 = bf16[128,1152]{1,0:T(8,128)(2,1)S(1)} fusion(f32[128,1152]{1,0:T(8,128)S(1)} %get-tuple-element.158, bf16[128,2304]{0,1:T(8,128)(2,1)S(1)} %multiply_convert_fusion, bf16[2304,1152]{1,0:T(8,128)(2,1)} %all-gather.3.cloned.1.call-done, bf16[128,1152]{1,0:T(8,128)(2,1)} %param.8), kind=kOutput, calls=%fused_computation.26 | convolution fusion | flops 682721280 | bytes 7077888 | tf_op jit(solution)/shard_map/dot_general | solution.py:24
  162.7 0.0 slice-done
  162.7 0.0 slice-done.1
  162.7 0.0 copy-start.1
  162.7 1.6 fusion.23
  164.3 0.9 copy-done.1
  165.2 1.6 fusion.7
  166.8 1.1 copy.14
  167.9 0.0 reduce-scatter.4.cloned.1.call-update
  167.9 9.3 %all_gather.19 = bf16[256,1152]{1,0:T(8,128)(2,1)} all-gather(bf16[128,1152]{1,0:T(8,128)(2,1)S(1)} %get-tuple-element.157), channel_id=1, replica_groups=mesh['dp'=2,'tp'=4,'section'=4] {'dp'}, dimensions={0}, use_global_device_ids=true | all-gather | bytes 884736 | tf_op jit(solution)/shard_map/all_gather | solution.py:55
  177.2 8.5 %all_gather.18 = bf16[256,1152]{1,0:T(8,128)(2,1)} all-gather(bf16[128,1152]{1,0:T(8,128)(2,1)S(1)} %fusion.15), channel_id=1, replica_groups=mesh['dp'=2,'tp'=4,'section'=4] {'dp'}, dimensions={0}, use_global_device_ids=true | all-gather | bytes 884736 | tf_op jit(solution)/shard_map/all_gather | solution.py:54
  185.7 0.0 all-to-all-done
  185.7 27.0 %while.16 = (s32[]{:T(128)}, f32[1152,1152]{1,0:T(8,128)}, f32[1152,1152]{1,0:T(8,128)}, bf16[256,1152]{1,0:T(8,128)(2,1)S(1)}, bf16[256,1152]{1,0:T(8,128)(2,1)...) while((s32[]{:T(128)}, f32[1152,1152]{1,0:T(8,128)}, ...), condition=%wide.region_7.0_spmd.clone, body=%wide.region_6.0_spmd.clone.sunk | while | flops 690094080 | bytes 33032356 | solution.py:77
  185.7 1.8 convolution_convert_fusion.4
  187.6 3.4 %convolution_convert_fusion.5 = bf16[1152,1152]{1,0:T(8,128)(2,1)} fusion(bf16[256,1152]{1,0:T(8,128)(2,1)} %get-tuple-element.224, s32[]{:T(128)S(6)} %select_n.16, bf16[256,1152]{1,0:T(8,128)(2,1)S(1)} %get-tuple-element.223), kind=kOutput, calls=%fused_computation.1.clone.1 | convolution fusion | flops 341065728 | bytes 3245056 | tf_op jit(solution)/shard_map/while/body/eval_jaxpr/dot_general | solution.py:63
  190.9 6.7 %select_add_fusion.3 = (f32[1152,1152]{1,0:T(8,128)}, f32[1152,1152]{1,0:T(8,128)}) fusion(f32[1152,1152]{1,0:T(8,128)} %get-tuple-element.212, bf16[1152,1152]{1,0:T(8,128)(2,1)S(1)} %convolution_convert_fusion.4, pred[]{:T(512)S(6)} %compare.3, bf16[1152,1152]{1,0:T(8,128)(2,1)} %convolution_convert_fusion.5, f32[1152,1152]{1,0:T(8,128)} %get-tuple-element.211), kind=kLoop, calls=%fused_computation.2.clone.1 | loop fusion | flops 7962624 | bytes 26542080 | tf_op jit(solution)/shard_map/while/body/eval_jaxpr/add | solution.py:72
  197.6 1.8 convolution_convert_fusion.4
  199.5 3.4 %convolution_convert_fusion.5 = bf16[1152,1152]{1,0:T(8,128)(2,1)} fusion(bf16[256,1152]{1,0:T(8,128)(2,1)} %get-tuple-element.224, s32[]{:T(128)S(6)} %select_n.16, bf16[256,1152]{1,0:T(8,128)(2,1)S(1)} %get-tuple-element.223), kind=kOutput, calls=%fused_computation.1.clone.1 | convolution fusion | flops 341065728 | bytes 3245056 | tf_op jit(solution)/shard_map/while/body/eval_jaxpr/dot_general | solution.py:63
  202.8 9.9 %select_add_fusion.3 = (f32[1152,1152]{1,0:T(8,128)}, f32[1152,1152]{1,0:T(8,128)}) fusion(f32[1152,1152]{1,0:T(8,128)} %get-tuple-element.212, bf16[1152,1152]{1,0:T(8,128)(2,1)S(1)} %convolution_convert_fusion.4, pred[]{:T(512)S(6)} %compare.3, bf16[1152,1152]{1,0:T(8,128)(2,1)} %convolution_convert_fusion.5, f32[1152,1152]{1,0:T(8,128)} %get-tuple-element.211), kind=kLoop, calls=%fused_computation.2.clone.1 | loop fusion | flops 7962624 | bytes 26542080 | tf_op jit(solution)/shard_map/while/body/eval_jaxpr/add | solution.py:72
  212.7 4.4 %convert_element_type.68 = bf16[1152,1152]{1,0:T(8,128)(2,1)} convert(f32[1152,1152]{1,0:T(8,128)} %get-tuple-element.115) | non-fusion elementwise | flops 1327104 | bytes 7962624 | tf_op jit(solution)/shard_map/convert_element_type | solution.py:84
  217.1 0.2 copy-done
  217.3 1.8 convert_element_type.67
  219.1 3.0 %reduce-scatter.4.cloned.1.call-done = bf16[144,128]{1,0:T(8,128)(2,1)} async-done(((bf16[2304,128]{1,0:T(8,128)(2,1)}), bf16[144,128]{1,0:T(8,128)(2,1)}) %reduce-scatter.4.cloned.1.call-update) | async-done | bytes 36880 | tf_op jit(solution)/shard_map/reduce_scatter | solution.py:35
  222.1 1.1 fusion.20
  223.2 5.5 %psum.15 = f32[144]{0:T(256)} all-reduce(f32[144]{0:T(256)S(1)} %get-tuple-element.141), channel_id=1, replica_groups=mesh['dp'=2,'tp'=4,'section'=4] {'dp'}, use_global_device_ids=true, to_apply=%region_5.0 | all-reduce | flops 144 | bytes 1152 | tf_op jit(solution)/shard_map/psum | solution.py:44
  228.6 29.5 %psum.14 = f32[128]{0:T(128)S(1)} all-reduce(f32[128]{0:T(128)S(1)} %get-tuple-element.142), channel_id=1, replica_groups=mesh['dp'=2,'tp'=4,'section'=4] {'tp','section'}, use_global_device_ids=true, to_apply=%region_3.0 | all-reduce | flops 128 | bytes 1024 | tf_op jit(solution)/shard_map/psum | solution.py:45
  258.1 1.6 fusion.17
  (8 shorter events, 0.0 us)
Async XLA Ops:
  7.2 1.5 copy-start.3
  7.2 10.9 %copy-start.4 = (f32[2304]{0:T(1024)S(1)}, f32[2304]{0:T(1024)}, u32[]{:S(2)}) copy-start(f32[2304]{0:T(1024)} %param.9) | copy-start | bytes 27652
  7.2 80.7 %all-gather.5.cloned.1.call-start = ((), (), s32[]{:S(2)}) async-start(), calls=%async_computation.3 | async-start | bytes 7962624 | tf_op jit(solution)/shard_map/all_gather | solution.py:20
  7.9 80.0 %copy-start.2 = (bf16[128,1152]{1,0:T(8,128)(2,1)S(1)}, bf16[128,1152]{1,0:T(8,128)(2,1)}, u32[]{:S(2)}) copy-start(bf16[128,1152]{1,0:T(8,128)(2,1)} %param.8) | copy-start | bytes 884740
  7.9 150.8 %all-gather.3.cloned.1.call-start = ((), (), s32[]{:S(2)}) async-start(), calls=%async_computation.2 | async-start | bytes 7962624 | tf_op jit(solution)/shard_map/all_gather | solution.py:21
  19.5 166.2 %all-to-all-start = ((bf16[128,2,1152]{2,0,1:T(8,128)(2,1)}), bf16[128,2,1152]{2,0,1:T(8,128)(2,1)S(1)}, u32[]{:S(2)}, u32[]{:S(2)}) async-start(bf16[128,2,1152]{2,0,1:T(8,128)(2,1)} %copy.13), calls=%async_computation | async-start | bytes 1179648 | tf_op jit(solution)/shard_map/all_to_all | solution.py:51
  23.0 199.1 %reduce-scatter.4.cloned.1.call-start = ((), (), s32[]{:S(2)}) async-start(), calls=%async_computation.4 | async-start | bytes 626688 | tf_op jit(solution)/shard_map/reduce_scatter | solution.py:35
  87.9 74.8 %slice-start = ((s8[5308416]{0:T(1024)(128)(4,1)}), s8[1114112]{0:T(1024)(128)(4,1)S(1)}, s32[]{:S(2)}) async-start(s8[5308416]{0:T(1024)(128)(4,1)} %bitcast.30), calls=%async_computation.5 | async-start | bytes 2228224
  158.7 4.0 %slice-start.1 = ((s8[5308416]{0:T(1024)(128)(4,1)}), s8[4194304]{0:T(1024)(128)(4,1)S(1)}, s32[]{:S(2)}) async-start(s8[5308416]{0:T(1024)(128)(4,1)} %bitcast.30), calls=%async_computation.6 | async-start | bytes 8388608
  162.7 2.5 copy-start.1
  212.7 4.7 %copy-start = (f32[1152,1152]{1,0:T(8,128)S(1)}, f32[1152,1152]{1,0:T(8,128)}, u32[]{:S(2)}) copy-start(f32[1152,1152]{1,0:T(8,128)} %get-tuple-element.114) | copy-start | bytes 15925252
Sparse Core Ops, SparseCore 0:
  9.5 78.3 all-gather.4
  89.4 69.2 all-gather.2
  168.0 54.0 reduce-scatter.3
where the time goes:
time: 267 us; the launch traced here: 266 us
  waiting for transfers between devices  135 us (51%)
  blocking collectives  61.8 us (23%)
  other arithmetic  27.3 us (10%)
  matrix products  21.2 us (8%)
  between operations  13.9 us (5%)
  starting transfers between devices  3.64 us (1%)
  local copies, waits for them, and re-layouts  3.38 us (1%)
    all_gather x1, waiting for transfers between devices, shards(): lax.all_gather(w_up, 'dp', axis=0, tiled=True)  67.1 us
    all_gather x1, waiting for transfers between devices, shards(): lax.all_gather(w_gate, 'dp', axis=0, tiled=True)  63.6 us
    psum x1, blocking collectives, shards(): row_sum = lax.psum(row_part, ('tp', 'section'))  29.5 us
    add x2, other arithmetic, one_block(): total + lax.optimization_barrier(term.astype(jnp.bfloat16)).astype(jnp.fl...  16.6 us
    all_gather x1, blocking collectives, shards(): piece_up = lax.all_gather(d_up, 'dp', axis=0, tiled=True)  9.34 us
    all_gather x1, blocking collectives, shards(): rows_in = lax.all_gather(tokens, 'section', axis=1, tiled=True)  9.03 us
    all_gather x1, blocking collectives, shards(): piece_gate = lax.all_gather(d_gate, 'dp', axis=0, tiled=True)  8.47 us
    dot_general x2, matrix products, one_block(): lax.dot_general(block_normed, block_gate, contract_rows, preferred_elemen...  6.71 us
  transfers between devices with their start and end apart: 4, of which 3 were waited for; matrix products, arithmetic and copies ran while one was open for 18% of the time, Pallas kernels for 0%

commit v1 on v0

--- a/solution.py
+++ b/solution.py
@@ -42,7 +42,7 @@
     gain_part = jnp.sum(d_normed * own_inputs * inv_rms[:, None], axis=0)
     row_part = jnp.sum(own_inputs * own_gain * d_normed, axis=1)
     grad_gain = lax.psum(gain_part, "dp")
-    row_sum = lax.psum(row_part, ("tp", "section"))
+    row_sum = lax.psum(lax.psum(row_part, "section"), "tp")
     grad_tokens = (
         inv_rms[:, None] * own_gain * d_normed - own_inputs * (inv_rms**3 * row_sum / D)[:, None]
     )

time: 267 us -> 254 us (0.951)
  blocking collectives: 61.8 us -> 48.9 us
    psum x1 -> x2, blocking collectives: 29.5 us -> 16.6 us  [shards(): row_sum = lax.psum(lax.psum(row_part, 'section'), 'tp')]
  transfers between devices with their start and end apart: 4 -> 4, of which waited for: 3 -> 3; matrix products, arithmetic and copies ran while one was open for 18% -> 19% of each run, Pallas kernels for 0% -> 0%
where the time goes in v1:
time: 254 us; the launch traced here: 253 us
  waiting for transfers between devices  135 us (53%)
  blocking collectives  48.9 us (19%)
  other arithmetic  27.3 us (11%)
  matrix products  21.2 us (8%)
  between operations  13.9 us (5%)
  starting transfers between devices  3.64 us (1%)
  local copies, waits for them, and re-layouts  3.38 us (1%)
    all_gather x1, waiting for transfers between devices, shards(): lax.all_gather(w_up, 'dp', axis=0, tiled=True)  67.1 us
    all_gather x1, waiting for transfers between devices, shards(): lax.all_gather(w_gate, 'dp', axis=0, tiled=True)  63.6 us
    add x2, other arithmetic, one_block(): total + lax.optimization_barrier(term.astype(jnp.bfloat16)).astype(jnp.fl...  16.6 us
    psum x2, blocking collectives, shards(): row_sum = lax.psum(lax.psum(row_part, 'section'), 'tp')  16.6 us
    all_gather x1, blocking collectives, shards(): piece_up = lax.all_gather(d_up, 'dp', axis=0, tiled=True)  9.34 us
    all_gather x1, blocking collectives, shards(): rows_in = lax.all_gather(tokens, 'section', axis=1, tiled=True)  9.03 us
    all_gather x1, blocking collectives, shards(): piece_gate = lax.all_gather(d_gate, 'dp', axis=0, tiled=True)  8.47 us
    dot_general x2, matrix products, one_block(): lax.dot_general(block_normed, block_gate, contract_rows, preferred_elemen...  6.71 us
  transfers between devices with their start and end apart: 4, of which 3 were waited for; matrix products, arithmetic and copies ran while one was open for 19% of the time, Pallas kernels for 0%

profile of v1, /device:TPU:0, one launch (start us, length us, event | category | flops | bytes accessed | tf_op | source)
XLA Modules:
  0.0 253.4 jit_solution(2131282536964239920)
XLA Ops:
  7.2 0.0 copy-start.3
  7.2 0.0 copy-start.4
  7.2 0.0 all-gather.5.cloned.1.call-start
  7.2 0.7 all-gather.5.cloned.1.call-update
  7.9 0.0 copy-start.2
  7.9 0.0 all-gather.3.cloned.1.call-start
  8.0 0.7 all-gather.3.cloned.1.call-update
  8.7 0.0 copy-done.3
  8.7 9.0 %all_gather.15 = bf16[128,2304]{0,1:T(8,128)(2,1)S(1)} all-gather(bf16[128,576]{0,1:T(8,128)(2,1)S(1)} %copy-done.3), channel_id=1, replica_groups=mesh['dp'=2,'tp'=4,'section'=4] {'section'}, dimensions={1}, use_global_device_ids=true | all-gather | bytes 737280 | tf_op jit(solution)/shard_map/all_gather | solution.py:15
  17.7 0.3 multiply_reduce_fusion
  18.1 0.0 copy-done.4
  18.1 0.4 multiply_convert_fusion
  18.4 1.1 copy.13
  19.5 3.5 %all-to-all-start = ((bf16[128,2,1152]{2,0,1:T(8,128)(2,1)}), bf16[128,2,1152]{2,0,1:T(8,128)(2,1)S(1)}, u32[]{:S(2)}, u32[]{:S(2)}) async-start(bf16[128,2,1152]{2,0,1:T(8,128)(2,1)} %copy.13), calls=%async_computation | async-start | bytes 1179648 | tf_op jit(solution)/shard_map/all_to_all | solution.py:51
  23.0 0.0 reduce-scatter.4.cloned.1.call-start
  23.1 1.1 convert_element_type.59
  24.2 0.1 dynamic_slice.27
  24.3 63.6 %all-gather.5.cloned.1.call-done = bf16[2304,1152]{1,0:T(8,128)(2,1)} async-done(((bf16[1152,1152]{1,0:T(8,128)(2,1)}), bf16[2304,1152]{1,0:T(8,128)(2,1)}) %all-gather.5.cloned.1.call-update) | async-done | bytes 5308432 | tf_op jit(solution)/shard_map/all_gather | solution.py:20
  87.9 0.0 copy-done.2
  87.9 3.7 %fusion.8 = (bf16[128,1152]{1,0:T(8,128)(2,1)S(1)}, f32[128,1152]{1,0:T(8,128)S(1)}) fusion(bf16[128,1152]{1,0:T(8,128)(2,1)S(1)} %copy-done.2, bf16[128,2304]{0,1:T(8,128)(2,1)S(1)} %multiply_convert_fusion, bf16[2304,1152]{1,0:T(8,128)(2,1)} %all-gather.5.cloned.1.call-done), kind=kOutput, calls=%fused_computation.19 | convolution fusion | flops 681099264 | bytes 7077888 | tf_op jit(solution)/shard_map/dot_general | solution.py:23
  91.6 67.1 %all-gather.3.cloned.1.call-done = bf16[2304,1152]{1,0:T(8,128)(2,1)} async-done(((bf16[1152,1152]{1,0:T(8,128)(2,1)}), bf16[2304,1152]{1,0:T(8,128)(2,1)}) %all-gather.3.cloned.1.call-update) | async-done | bytes 5308432 | tf_op jit(solution)/shard_map/all_gather | solution.py:21
  158.7 4.0 %fusion.15 = bf16[128,1152]{1,0:T(8,128)(2,1)S(1)} fusion(f32[128,1152]{1,0:T(8,128)S(1)} %get-tuple-element.158, bf16[128,2304]{0,1:T(8,128)(2,1)S(1)} %multiply_convert_fusion, bf16[2304,1152]{1,0:T(8,128)(2,1)} %all-gather.3.cloned.1.call-done, bf16[128,1152]{1,0:T(8,128)(2,1)} %param.8), kind=kOutput, calls=%fused_computation.26 | convolution fusion | flops 682721280 | bytes 7077888 | tf_op jit(solution)/shard_map/dot_general | solution.py:24
  162.7 0.0 slice-done
  162.7 0.0 slice-done.1
  162.7 1.6 fusion.23
  164.3 0.9 copy-done.1
  165.2 1.6 fusion.7
  166.8 1.1 copy.14
  167.9 0.0 reduce-scatter.4.cloned.1.call-update
  167.9 9.3 %all_gather.19 = bf16[256,1152]{1,0:T(8,128)(2,1)} all-gather(bf16[128,1152]{1,0:T(8,128)(2,1)S(1)} %get-tuple-element.157), channel_id=1, replica_groups=mesh['dp'=2,'tp'=4,'section'=4] {'dp'}, dimensions={0}, use_global_device_ids=true | all-gather | bytes 884736 | tf_op jit(solution)/shard_map/all_gather | solution.py:55
  177.2 8.5 %all_gather.18 = bf16[256,1152]{1,0:T(8,128)(2,1)} all-gather(bf16[128,1152]{1,0:T(8,128)(2,1)S(1)} %fusion.15), channel_id=1, replica_groups=mesh['dp'=2,'tp'=4,'section'=4] {'dp'}, dimensions={0}, use_global_device_ids=true | all-gather | bytes 884736 | tf_op jit(solution)/shard_map/all_gather | solution.py:54
  185.7 0.0 all-to-all-done
  185.7 27.0 %while.16 = (s32[]{:T(128)}, f32[1152,1152]{1,0:T(8,128)}, f32[1152,1152]{1,0:T(8,128)}, bf16[256,1152]{1,0:T(8,128)(2,1)S(1)}, bf16[256,1152]{1,0:T(8,128)(2,1)...) while((s32[]{:T(128)}, f32[1152,1152]{1,0:T(8,128)}, ...), condition=%wide.region_8.0_spmd.clone, body=%wide.region_7.0_spmd.clone.sunk | while | flops 690094080 | bytes 33032356 | solution.py:77
  185.7 1.8 convolution_convert_fusion.4
  187.6 3.4 %convolution_convert_fusion.5 = bf16[1152,1152]{1,0:T(8,128)(2,1)} fusion(bf16[256,1152]{1,0:T(8,128)(2,1)} %get-tuple-element.224, s32[]{:T(128)S(6)} %select_n.16, bf16[256,1152]{1,0:T(8,128)(2,1)S(1)} %get-tuple-element.223), kind=kOutput, calls=%fused_computation.1.clone.1 | convolution fusion | flops 341065728 | bytes 3245056 | tf_op jit(solution)/shard_map/while/body/eval_jaxpr/dot_general | solution.py:63
  190.9 6.7 %select_add_fusion.3 = (f32[1152,1152]{1,0:T(8,128)}, f32[1152,1152]{1,0:T(8,128)}) fusion(f32[1152,1152]{1,0:T(8,128)} %get-tuple-element.212, bf16[1152,1152]{1,0:T(8,128)(2,1)S(1)} %convolution_convert_fusion.4, pred[]{:T(512)S(6)} %compare.3, bf16[1152,1152]{1,0:T(8,128)(2,1)} %convolution_convert_fusion.5, f32[1152,1152]{1,0:T(8,128)} %get-tuple-element.211), kind=kLoop, calls=%fused_computation.2.clone.1 | loop fusion | flops 7962624 | bytes 26542080 | tf_op jit(solution)/shard_map/while/body/eval_jaxpr/add | solution.py:72
  197.6 1.8 convolution_convert_fusion.4
  199.5 3.4 %convolution_convert_fusion.5 = bf16[1152,1152]{1,0:T(8,128)(2,1)} fusion(bf16[256,1152]{1,0:T(8,128)(2,1)} %get-tuple-element.224, s32[]{:T(128)S(6)} %select_n.16, bf16[256,1152]{1,0:T(8,128)(2,1)S(1)} %get-tuple-element.223), kind=kOutput, calls=%fused_computation.1.clone.1 | convolution fusion | flops 341065728 | bytes 3245056 | tf_op jit(solution)/shard_map/while/body/eval_jaxpr/dot_general | solution.py:63
  202.8 9.9 %select_add_fusion.3 = (f32[1152,1152]{1,0:T(8,128)}, f32[1152,1152]{1,0:T(8,128)}) fusion(f32[1152,1152]{1,0:T(8,128)} %get-tuple-element.212, bf16[1152,1152]{1,0:T(8,128)(2,1)S(1)} %convolution_convert_fusion.4, pred[]{:T(512)S(6)} %compare.3, bf16[1152,1152]{1,0:T(8,128)(2,1)} %convolution_convert_fusion.5, f32[1152,1152]{1,0:T(8,128)} %get-tuple-element.211), kind=kLoop, calls=%fused_computation.2.clone.1 | loop fusion | flops 7962624 | bytes 26542080 | tf_op jit(solution)/shard_map/while/body/eval_jaxpr/add | solution.py:72
  212.7 4.4 %convert_element_type.68 = bf16[1152,1152]{1,0:T(8,128)(2,1)} convert(f32[1152,1152]{1,0:T(8,128)} %get-tuple-element.115) | non-fusion elementwise | flops 1327104 | bytes 7962624 | tf_op jit(solution)/shard_map/convert_element_type | solution.py:84
  217.2 0.2 copy-done
  217.4 1.8 convert_element_type.67
  219.2 2.9 %reduce-scatter.4.cloned.1.call-done = bf16[144,128]{1,0:T(8,128)(2,1)} async-done(((bf16[2304,128]{1,0:T(8,128)(2,1)}), bf16[144,128]{1,0:T(8,128)(2,1)}) %reduce-scatter.4.cloned.1.call-update) | async-done | bytes 36880 | tf_op jit(solution)/shard_map/reduce_scatter | solution.py:35
  222.1 1.1 fusion.20
  223.2 5.5 %psum.23 = f32[144]{0:T(256)} all-reduce(f32[144]{0:T(256)S(1)} %get-tuple-element.141), channel_id=1, replica_groups=mesh['dp'=2,'tp'=4,'section'=4] {'dp'}, use_global_device_ids=true, to_apply=%region_6.0 | all-reduce | flops 144 | bytes 1152 | tf_op jit(solution)/shard_map/psum | solution.py:44
  228.6 5.6 %psum.21 = f32[128]{0:T(128)S(1)} all-reduce(f32[128]{0:T(128)S(1)} %get-tuple-element.142), channel_id=1, replica_groups=mesh['dp'=2,'tp'=4,'section'=4] {'section'}, use_global_device_ids=true, to_apply=%region_3.0 | all-reduce | flops 128 | bytes 1024 | tf_op jit(solution)/shard_map/psum | solution.py:45
  234.3 10.9 %psum.22 = f32[128]{0:T(128)S(1)} all-reduce(f32[128]{0:T(128)S(1)} %psum.21), channel_id=1, replica_groups=mesh['dp'=2,'tp'=4,'section'=4] {'tp'}, use_global_device_ids=true, to_apply=%region_4.0 | all-reduce | flops 128 | bytes 1024 | tf_op jit(solution)/shard_map/psum | solution.py:45
  245.2 1.6 fusion.17
  (9 shorter events, 0.0 us)
Async XLA Ops:
  7.2 1.5 copy-start.3
  7.2 10.9 %copy-start.4 = (f32[2304]{0:T(1024)S(1)}, f32[2304]{0:T(1024)}, u32[]{:S(2)}) copy-start(f32[2304]{0:T(1024)} %param.9) | copy-start | bytes 27652
  7.2 80.7 %all-gather.5.cloned.1.call-start = ((), (), s32[]{:S(2)}) async-start(), calls=%async_computation.3 | async-start | bytes 7962624 | tf_op jit(solution)/shard_map/all_gather | solution.py:20
  7.9 80.0 %copy-start.2 = (bf16[128,1152]{1,0:T(8,128)(2,1)S(1)}, bf16[128,1152]{1,0:T(8,128)(2,1)}, u32[]{:S(2)}) copy-start(bf16[128,1152]{1,0:T(8,128)(2,1)} %param.8) | copy-start | bytes 884740
  7.9 150.8 %all-gather.3.cloned.1.call-start = ((), (), s32[]{:S(2)}) async-start(), calls=%async_computation.2 | async-start | bytes 7962624 | tf_op jit(solution)/shard_map/all_gather | solution.py:21
  19.5 166.2 %all-to-all-start = ((bf16[128,2,1152]{2,0,1:T(8,128)(2,1)}), bf16[128,2,1152]{2,0,1:T(8,128)(2,1)S(1)}, u32[]{:S(2)}, u32[]{:S(2)}) async-start(bf16[128,2,1152]{2,0,1:T(8,128)(2,1)} %copy.13), calls=%async_computation | async-start | bytes 1179648 | tf_op jit(solution)/shard_map/all_to_all | solution.py:51
  23.0 199.1 %reduce-scatter.4.cloned.1.call-start = ((), (), s32[]{:S(2)}) async-start(), calls=%async_computation.4 | async-start | bytes 626688 | tf_op jit(solution)/shard_map/reduce_scatter | solution.py:35
  87.9 74.8 %slice-start = ((s8[5308416]{0:T(1024)(128)(4,1)}), s8[1114112]{0:T(1024)(128)(4,1)S(1)}, s32[]{:S(2)}) async-start(s8[5308416]{0:T(1024)(128)(4,1)} %bitcast.30), calls=%async_computation.5 | async-start | bytes 2228224
  158.7 4.0 %slice-start.1 = ((s8[5308416]{0:T(1024)(128)(4,1)}), s8[4194304]{0:T(1024)(128)(4,1)S(1)}, s32[]{:S(2)}) async-start(s8[5308416]{0:T(1024)(128)(4,1)} %bitcast.30), calls=%async_computation.6 | async-start | bytes 8388608
  162.7 2.5 copy-start.1
  212.7 4.7 %copy-start = (f32[1152,1152]{1,0:T(8,128)S(1)}, f32[1152,1152]{1,0:T(8,128)}, u32[]{:S(2)}) copy-start(f32[1152,1152]{1,0:T(8,128)} %get-tuple-element.114) | copy-start | bytes 15925252
Sparse Core Ops, SparseCore 0:
  9.5 78.3 all-gather.4
  89.4 69.2 all-gather.2
  168.0 54.0 reduce-scatter.3
